TPU v7x, 32 devices: a whole 2x2x4 slice. The times are simulated.
32 devices in a mesh: row: 8 (over z, x), col: 4 (over y, core).
Axes of the slice: x: 2, y: 2, z: 4, core: 2. Of those that a mesh axis runs over, the one named last changes fastest.
Arguments:
- gradients: bfloat16 [8, 4, 4, 64, 1536], P('row', 'col'), may hold values from -96 to 96
- token_counts: int32 [8, 4], P('row', 'col'), may hold values from 16 to 256
- row_groups: int32 [2, 8, 4], replicated, may hold values from 0 to 3, each once within a row
- col_groups: int32 [1, 4, 8], replicated, may hold values from 0 to 7, each once within a row
Outputs:
- averaged: float32 [8, 4, 4, 64, 1536], P('row', 'col')
- totals: int32 [8, 4], P('row', 'col')
Inputs may be any that keep to these rules, and one draw needn't show every extreme that they name: row_groups[r, i] lists the 4 grid columns in some order: in row round r, grid row i's member of group g sits in column row_groups[r, i, g]. col_groups[0, j] lists the 8 grid rows in some order: grid column j's member of group h sits in row col_groups[0, j, h].
All inputs are finite; a program needn't handle non-finite values.
Results may differ from a plain program's by a relative error of at most 0.0003.
Values may be sent and summed in bfloat16 or wider, within the bound.
No kernel may reach another device: no remote copies, remote signals or barrier semaphores. Data moves between devices by JAX's collectives and lax.ppermute only.
A program may use at most 64 MiB of HBM per device.

v0:
```python
import jax
import jax.numpy as jnp
from jax import lax
from jax.sharding import PartitionSpec as P


def weigh_groups(pieces, weights, group_order):
    scaled = pieces * weights[:, None, None]
    return (jnp.take(scaled, group_order, axis=0), jnp.take(weights, group_order, axis=0))


def return_order(averaged, weights, group_order):
    inverse = jnp.argsort(group_order)
    return (jnp.take(averaged, inverse, axis=0), jnp.take(weights, inverse, axis=0))


def opening_spread(gradients, weight):
    members = lax.axis_size("col")
    pieces = gradients.reshape(members, -1, gradients.shape[-1])
    spread = jnp.full((members,), weight, jnp.float32).astype(jnp.bfloat16)
    arrived, arrived_w = (
        lax.all_to_all(pieces, "col", split_axis=0, concat_axis=0, tiled=True),
        lax.all_to_all(spread, "col", split_axis=0, concat_axis=0, tiled=True),
    )
    return (arrived.astype(jnp.float32), arrived_w.astype(jnp.float32))


def regroup(values, weights, index_table):
    groups = values.shape[0]
    selector = (
        index_table[:, :, None] == jnp.arange(groups, dtype=jnp.int32)[None, None, :]
    ).astype(jnp.float32)
    mixing = jnp.sum(selector, axis=1) * weights[None, :]
    flattened = values.reshape(groups, -1)
    numerator = jnp.dot(
        mixing, flattened, precision=lax.Precision.HIGHEST, preferred_element_type=jnp.float32
    )
    new_totals = jnp.sum(mixing, axis=1)
    mixed = numerator / new_totals[:, None]
    return (mixed.reshape((index_table.shape[0],) + values.shape[1:]), new_totals)


def local(gradients, token_counts, row_groups, col_groups):
    row_place = lax.axis_index("row")
    state_shape = (gradients.shape[2] * gradients.shape[3], gradients.shape[4])
    weight = token_counts.reshape(()).astype(jnp.float32)
    arrived, arrived_w = opening_spread(gradients, weight)
    members = lax.axis_size("col")
    row_count = lax.axis_size("row")
    ordered, group_w = weigh_groups(arrived, arrived_w, row_groups[0, row_place])
    first_inverse = jnp.argsort(row_groups[0], axis=1)
    column_ids = jnp.arange(members, dtype=jnp.int32)
    index_two = first_inverse[col_groups[0].T, column_ids[None, :]]
    second_inverse = jnp.argsort(col_groups[0], axis=1)
    row_ids = jnp.arange(row_count, dtype=jnp.int32)
    index_three = second_inverse[row_groups[1].T, row_ids[None, :]]
    group_sums, first_w = lax.psum((ordered, group_w), "row")
    first_avg = group_sums / first_w[:, None, None]
    second, second_w = regroup(first_avg, first_w, index_two)
    third_avg, third_w = regroup(second, second_w, index_three)
    outgoing, outgoing_w = return_order(third_avg, third_w, row_groups[1, row_place])
    returned, returned_w = (
        lax.all_to_all(outgoing, "col", split_axis=0, concat_axis=0, tiled=True),
        lax.all_to_all(outgoing_w, "col", split_axis=0, concat_axis=0, tiled=True),
    )
    grad_state = returned.reshape(state_shape)
    weight = returned_w[0]
    return (
        grad_state.reshape(gradients.shape),
        weight.astype(jnp.int32).reshape(token_counts.shape),
    )


def solution(mesh):
    placed = (P("row", "col", None, None, None), P("row", "col"), P(), P())
    return jax.shard_map(
        local,
        mesh=mesh,
        in_specs=placed,
        out_specs=(P("row", "col", None, None, None), P("row", "col")),
        check_vma=False,
    )
```

profile of v0, /device:TPU:0, one launch (start us, length us, event | category | flops | bytes accessed | tf_op | source)
XLA Modules:
  0.0 169.0 jit_solution(17245745571147319791)
XLA Ops:
  7.8 0.6 broadcast_in_dim.26
  8.4 4.3 %all-to-all-start = ((bf16[4,1,1]{2,1,0:T(2,128)(2,1)}), bf16[4,1,1]{2,1,0:T(2,128)(2,1)S(1)}, u32[]{:S(2)}, u32[]{:S(2)}) async-start(bf16[4,1,1]{2,1,0:T(2,128)(2,1)} %broadcast_in_dim.26), calls=%async_computation | async-start | bytes 4096 | tf_op jit(solution)/shard_map/all_to_all | solution.py:23
  12.7 0.9 dynamic-slice_reduce_fusion
  13.6 2.8 %all-to-all-done = bf16[4,1,1]{2,1,0:T(2,128)(2,1)S(1)} async-done(((bf16[4,1,1]{2,1,0:T(2,128)(2,1)}), bf16[4,1,1]{2,1,0:T(2,128)(2,1)S(1)}, u32[]{:S(2)}, u32[]{:S(2)}) %all-to-all-start) | async-done | bytes 40 | tf_op jit(solution)/shard_map/all_to_all | solution.py:23
  16.4 3.5 %all-to-all-start.1 = ((bf16[4,64,1536]{2,1,0:T(8,128)(2,1)}), bf16[4,64,1536]{2,1,0:T(8,128)(2,1)S(1)}, u32[]{:S(2)}, u32[]{:S(2)}) async-start(bf16[4,64,1536]{2,1,0:T(8,128)(2,1)} %bitcast.41), calls=%async_computation.1 | async-start | bytes 1572864 | tf_op jit(solution)/shard_map/all_to_all | solution.py:22
  20.1 0.6 gather_fusion.2
  20.7 10.7 %all-to-all-done.1 = bf16[4,64,1536]{2,1,0:T(8,128)(2,1)S(1)} async-done(((bf16[4,64,1536]{2,1,0:T(8,128)(2,1)}), bf16[4,64,1536]{2,1,0:T(8,128)(2,1)S(1)}, u32[]{:S(2)}, u32[]{:S(2)}) %all-to-all-start.1) | async-done | bytes 786464 | tf_op jit(solution)/shard_map/all_to_all | solution.py:22
  31.5 0.2 convert_multiply_fusion
  31.7 0.7 gather_fusion.3
  32.4 1.4 broadcast_select_fusion.1
  33.8 0.7 copy-done.1
  34.7 0.6 sort.52
  35.3 0.8 gather_fusion.1
  36.4 0.7 sort.51
  37.0 0.7 gather_fusion
  37.8 0.8 sort.53
  38.7 22.8 %psum.14 = f32[4]{0:T(128)S(1)} all-reduce(f32[4]{0:T(128)S(1)} %get-tuple-element.14), channel_id=1, replica_groups=mesh['row'=8,'col'=4] {'row'}, use_global_device_ids=true, to_apply=%region_4.6 | all-reduce | flops 4 | bytes 32 | tf_op jit(solution)/shard_map/psum | solution.py:57
  61.7 0.6 gather_fusion.5
  62.3 0.7 copy.22
  63.0 3.2 %all-to-all-start.3 = ((f32[4,1,1]{2,1,0:T(1,128)}), f32[4,1,1]{2,1,0:T(1,128)S(1)}, u32[]{:S(2)}, u32[]{:S(2)}) async-start(f32[4,1,1]{2,1,0:T(1,128)} %copy.22), calls=%async_computation.3 | async-start | bytes 4096 | tf_op jit(solution)/shard_map/all_to_all | solution.py:64
  66.2 58.1 %all-reduce.2.cloned.1.call-done = f32[4,64,1536]{2,1,0:T(8,128)} async-done(((f32[4,64,1536]{2,1,0:T(8,128)}), f32[4,64,1536]{2,1,0:T(8,128)}) %all-reduce.2.cloned.1.call-update) | async-done | bytes 1572880 | tf_op jit(solution)/shard_map/psum | solution.py:57
  124.3 1.6 divide_bitcast_fusion
  125.9 1.0 copy.23
  127.0 3.9 %convolution_divide_fusion = f32[8,98304]{1,0:T(8,128)S(1)} fusion(f32[4,98304]{1,0:T(4,128)S(1)} %bitcast.40, f32[8]{0:T(128)S(1)} %multiply_reduce_fusion.1, f32[8,4]{0,1:T(4,128)S(1)} %convert_reduce_fusion.1, f32[4]{0:T(128)S(1)} %psum.14), kind=kOutput, calls=%fused_computation.6 | convolution fusion | flops 38535200 | bytes 4718768 | tf_op jit(solution)/shard_map/dot_general | solution.py:35
  130.9 2.8 %convolution_divide_fusion.1 = f32[4,98304]{1,0:T(4,128)S(1)} fusion(f32[8,98304]{1,0:T(8,128)S(1)} %convolution_divide_fusion, f32[4]{0:T(128)S(1)} %multiply_reduce_fusion, f32[4,8]{1,0:T(4,128)S(1)} %convert_reduce_fusion, f32[8]{0:T(128)S(1)} %multiply_reduce_fusion.1), kind=kOutput, calls=%fused_computation.7 | convolution fusion | flops 38141984 | bytes 4718768 | tf_op jit(solution)/shard_map/dot_general | solution.py:35
  133.7 0.5 copy.26
  134.2 0.7 gather_fusion.4
  134.9 1.4 broadcast_select_fusion
  136.3 3.6 %all-to-all-start.2 = ((f32[4,64,1536]{2,1,0:T(8,128)}), f32[4,64,1536]{2,1,0:T(8,128)S(1)}, u32[]{:S(2)}, u32[]{:S(2)}) async-start(f32[4,64,1536]{2,1,0:T(8,128)} %broadcast_select_fusion), calls=%async_computation.2 | async-start | bytes 3145728 | tf_op jit(solution)/shard_map/all_to_all | solution.py:63
  139.9 0.6 slice.25
  141.1 18.7 %all-to-all-done.2 = f32[4,64,1536]{2,1,0:T(8,128)S(1)} async-done(((f32[4,64,1536]{2,1,0:T(8,128)}), f32[4,64,1536]{2,1,0:T(8,128)S(1)}, u32[]{:S(2)}, u32[]{:S(2)}) %all-to-all-start.2) | async-done | bytes 1572896 | tf_op jit(solution)/shard_map/all_to_all | solution.py:63
  159.9 1.1 copy.30
  (30 shorter events, 1.1 us)
Async XLA Ops:
  8.4 8.0 %all-to-all-start = ((bf16[4,1,1]{2,1,0:T(2,128)(2,1)}), bf16[4,1,1]{2,1,0:T(2,128)(2,1)S(1)}, u32[]{:S(2)}, u32[]{:S(2)}) async-start(bf16[4,1,1]{2,1,0:T(2,128)(2,1)} %broadcast_in_dim.26), calls=%async_computation | async-start | bytes 4096 | tf_op jit(solution)/shard_map/all_to_all | solution.py:23
  16.4 15.1 %all-to-all-start.1 = ((bf16[4,64,1536]{2,1,0:T(8,128)(2,1)}), bf16[4,64,1536]{2,1,0:T(8,128)(2,1)S(1)}, u32[]{:S(2)}, u32[]{:S(2)}) async-start(bf16[4,64,1536]{2,1,0:T(8,128)(2,1)} %bitcast.41), calls=%async_computation.1 | async-start | bytes 1572864 | tf_op jit(solution)/shard_map/all_to_all | solution.py:22
  19.9 104.4 %all-reduce.2.cloned.1.call-start = ((), (), s32[]{:S(2)}) async-start(), calls=%async_computation.4 | async-start | bytes 3145728 | tf_op jit(solution)/shard_map/psum | solution.py:57
  33.8 0.7 copy-start.1
  33.8 0.9 copy-start
  63.0 73.3 %all-to-all-start.3 = ((f32[4,1,1]{2,1,0:T(1,128)}), f32[4,1,1]{2,1,0:T(1,128)S(1)}, u32[]{:S(2)}, u32[]{:S(2)}) async-start(f32[4,1,1]{2,1,0:T(1,128)} %copy.22), calls=%async_computation.3 | async-start | bytes 4096 | tf_op jit(solution)/shard_map/all_to_all | solution.py:64
  136.3 23.6 %all-to-all-start.2 = ((f32[4,64,1536]{2,1,0:T(8,128)}), f32[4,64,1536]{2,1,0:T(8,128)S(1)}, u32[]{:S(2)}, u32[]{:S(2)}) async-start(f32[4,64,1536]{2,1,0:T(8,128)} %broadcast_select_fusion), calls=%async_computation.2 | async-start | bytes 3145728 | tf_op jit(solution)/shard_map/all_to_all | solution.py:63
Sparse Core Ops, SparseCore 0:
  33.9 90.3 all-reduce.1
where the time goes:
time: 169 us
  waiting for transfers between devices  90.4 us (53%)
  blocking collectives  22.8 us (13%)
  between operations  16.6 us (10%)
  starting transfers between devices  14.6 us (9%)
  local copies, waits for them, and re-layouts  10.7 us (6%)
  other arithmetic  7.22 us (4%)
  matrix products  6.72 us (4%)
    psum x1, waiting for transfers between devices, local(): group_sums, first_w = lax.psum((ordered, group_w), 'row')  58.1 us
    psum x1, blocking collectives, local(): group_sums, first_w = lax.psum((ordered, group_w), 'row')  22.8 us
    all_to_all x1, waiting for transfers between devices, local(): lax.all_to_all(outgoing, 'col', split_axis=0, concat_axis=0, tiled=True)  18.7 us
    all_to_all x1, waiting for transfers between devices, opening_spread(): lax.all_to_all(pieces, 'col', split_axis=0, concat_axis=0, tiled=True)  10.7 us
    dot_general x2, matrix products, regroup(): jnp.dot(mixing, flattened, precision=lax.Precision.HIGHEST, preferred_ele...  6.72 us
    all_to_all x1, starting transfers between devices, opening_spread(): lax.all_to_all(spread, 'col', split_axis=0, concat_axis=0, tiled=True)  4.26 us
    all_to_all x1, starting transfers between devices, local(): lax.all_to_all(outgoing, 'col', split_axis=0, concat_axis=0, tiled=True)  3.56 us
    all_to_all x1, starting transfers between devices, opening_spread(): lax.all_to_all(pieces, 'col', split_axis=0, concat_axis=0, tiled=True)  3.5 us
  transfers between devices with their start and end apart: 5, of which 4 were waited for; matrix products, arithmetic and copies ran while one was open for 12% of the time, Pallas kernels for 0%

commit v1 on v0

v1 whole, which is shorter than its diff:
```python
import functools

import jax
import jax.numpy as jnp
from jax import lax
from jax.experimental import pallas as pl
from jax.experimental.pallas import tpu as pltpu
from jax.sharding import PartitionSpec as P

GRID = ("row", "col")
TOP = 60000.0
TAIL = 128
CUTS = 4
SMEM = pl.BlockSpec(memory_space=pltpu.SMEM)
VMEM = pl.BlockSpec(memory_space=pltpu.VMEM)
ROOM = pltpu.CompilerParams(vmem_limit_bytes=16 * 2**20)


def one_hot(values, count):
    return (values[..., None] == jnp.arange(count, dtype=jnp.int32)).astype(jnp.float32)


def path_counts(row_groups, col_groups):
    rows, cols = row_groups.shape[1:]
    first = one_hot(row_groups[0], cols)
    second = one_hot(col_groups[0], rows)
    third = one_hot(row_groups[1], cols)
    exact = functools.partial(jnp.einsum, precision=lax.Precision.HIGHEST)
    two = exact("jhi,igj->hg", second, first)
    three = exact("ikj,jhi->kh", third, second)
    paths = exact("kg,igj->kij", exact("kh,hg->kg", three, two), first)
    numbers = jnp.arange(cols, dtype=jnp.float32)[None, :, None]
    group_of = jnp.sum(third * numbers, axis=1).astype(jnp.int32)
    return paths.reshape(cols, rows * cols), group_of.reshape(-1)


def pack_kernel(count, gradients, out, sems):
    height, width = gradients.shape
    cut = height // CUTS
    copies = []
    for n in range(CUTS):
        part = pl.ds(n * cut, cut)
        copy = pltpu.make_async_copy(
            gradients.at[part, :], out.at[part, pl.ds(0, width)], sems.at[n]
        )
        copy.start()
        copies.append(copy)
    peak = jnp.zeros((1, width), jnp.float32)
    for n, copy in enumerate(copies):
        copy.wait()
        x = out[pl.ds(n * cut, cut), pl.ds(0, width)].astype(jnp.float32)
        peak = jnp.maximum(peak, jnp.max(jnp.abs(x), axis=0, keepdims=True))
    highest = jnp.max(peak, axis=1, keepdims=True)
    lane = lax.broadcasted_iota(jnp.int32, (height, TAIL), 1)
    tail = jnp.where(lane < TAIL // 2, count[0].astype(jnp.float32), highest)
    out[:, pl.ds(width, TAIL)] = tail.astype(out.dtype)


def mix_kernel(paths, pieces, coded, facts):
    groups, replicas = paths.shape
    step = 4 if replicas % 4 == 0 else 1
    width = pieces.shape[2] - TAIL
    height = pieces.shape[1]
    lanes = width // 2 if width % 256 == 0 else width
    for k0 in range(0, groups, 4):
        ks = range(k0, min(k0 + 4, groups))
        for c in range(0, width, lanes):

            def body(s, held):
                for u in range(step):
                    at = s * step + u
                    x = pieces[at, :, c:c + lanes].astype(jnp.float32)
                    tail = pieces[at, :, width:].astype(jnp.float32)
                    w, m = tail[:, :1], tail[:, TAIL - 1:]
                    sums, totals, bounds = held
                    shares = tuple(paths[k, at] * w for k in ks)
                    sums = tuple(a + q * x for a, q in zip(sums, shares))
                    totals = tuple(a + q for a, q in zip(totals, shares))
                    bounds = tuple(a + q * m for a, q in zip(bounds, shares))
                    held = (sums, totals, bounds)
                return held

            def zeros(wide):
                return tuple(jnp.zeros((height, wide), jnp.float32) for _ in ks)

            start = (zeros(lanes), zeros(1), zeros(1))
            sums, totals, bounds = lax.fori_loop(0, replicas // step, body, start)
            for a, t, b, k in zip(sums, totals, bounds, ks):
                unit = a * jnp.where(b > 0.0, 1.0 / b, 0.0)
                coded[k, :, c:c + lanes] = unit * jnp.abs(unit) * TOP
                lane = lax.broadcasted_iota(jnp.int32, (height, TAIL), 1)
                facts[k] = jnp.where(lane == 0, t, b / t)


def local(gradients, token_counts, row_groups, col_groups):
    rows, cols = lax.axis_size("row"), lax.axis_size("col")
    replicas = rows * cols
    place = lax.axis_index("row") * cols + lax.axis_index("col")
    width = gradients.shape[-1]
    flat = gradients.reshape(-1, width)
    packed = pl.pallas_call(
        pack_kernel,
        in_specs=[SMEM, pl.BlockSpec(memory_space=pl.ANY)],
        out_specs=VMEM,
        out_shape=jax.ShapeDtypeStruct((flat.shape[0], width + TAIL), flat.dtype),
        scratch_shapes=[pltpu.SemaphoreType.DMA((CUTS,))],
        compiler_params=ROOM,
    )(token_counts.reshape(1), flat)
    pieces = packed.reshape(replicas, -1, width + TAIL)
    arrived = lax.all_to_all(pieces, GRID, split_axis=0, concat_axis=0, tiled=True)
    height = arrived.shape[1]
    paths, group_of = path_counts(row_groups, col_groups)
    coded, facts = pl.pallas_call(
        mix_kernel,
        in_specs=[SMEM, VMEM],
        out_specs=(VMEM, VMEM),
        out_shape=(
            jax.ShapeDtypeStruct((cols, height, width), jnp.float32),
            jax.ShapeDtypeStruct((cols, height, TAIL), jnp.float32),
        ),
        compiler_params=ROOM,
    )(paths, arrived)
    chosen = coded[0][None]
    for k in range(1, cols):
        chosen = jnp.where((group_of == k)[:, None, None], coded[k][None], chosen)
    chosen = chosen.astype(jnp.float16)
    returned = lax.all_to_all(chosen, GRID, split_axis=0, concat_axis=0, tiled=True)
    own = (jnp.arange(cols) == group_of[place])[:, None]
    total, bound = jnp.sum(jnp.where(own, facts[:, 0, :2], 0.0), axis=0)
    code = returned.astype(jnp.float32)
    root = lax.rsqrt(jnp.maximum(jnp.abs(code), 1e-12))
    averaged = code * root * (bound * TOP ** -0.5)
    return (
        averaged.reshape(gradients.shape),
        total.astype(jnp.int32).reshape(token_counts.shape),
    )


def solution(mesh):
    placed = (P(*GRID, None, None, None), P(*GRID), P(), P())
    return jax.shard_map(
        local,
        mesh=mesh,
        in_specs=placed,
        out_specs=(P(*GRID, None, None, None), P(*GRID)),
        check_vma=False,
    )
```

time: 169 us -> 64.2 us (0.38)
  waiting for transfers between devices: 90.4 us -> 38.1 us
  blocking collectives: 22.8 us -> 0 us
  between operations: 16.6 us -> 3.77 us
  local copies, waits for them, and re-layouts: 10.7 us -> 2.85 us
  matrix products: 6.72 us -> 0.65 us
  Pallas kernels: 0 us -> 3.79 us
  starting transfers between devices: 14.6 us -> 11 us
  other arithmetic: 7.22 us -> 3.7 us
    psum x1 -> x0, waiting for transfers between devices: 58.1 us -> none  [local(): group_sums, first_w = lax.psum((ordered, group_w), 'row')]
    psum x1 -> x0, blocking collectives: 22.8 us -> none  [local(): group_sums, first_w = lax.psum((ordered, group_w), 'row')]
    dot_general x2 -> x4, matrix products: 6.72 us -> 0.65 us  [the longest x2 0.27 us: path_counts(): paths = exact('kg,igj->kij', exact('kh,hg->kg', three, two), first)]
    all_to_all x4 -> x2, waiting for transfers between devices: 32.3 us -> 38.1 us  [the longest x1 20.9 us: local(): lax.all_to_all(pieces, GRID, split_axis=0, concat_axis=0, tiled=True)]
    gather x9 -> x0, local copies, waits for them, and re-layouts: 4.26 us -> none  [the longest x3 0.92 us: local(): index_two = first_inverse[col_groups[0].T, column_ids[None, :]]]
    pallas_call x0 -> x2, Pallas kernels: none -> 3.79 us  [the longest x1 2.5 us: local(): pl.pallas_call(mix_kernel, in_specs=[SMEM, VMEM], out_specs=(VMEM, VMEM),...]
    all_to_all x4 -> x2, starting transfers between devices: 14.5 us -> 11 us  [the longest x1 7.33 us: local(): lax.all_to_all(pieces, GRID, split_axis=0, concat_axis=0, tiled=True)]
    select_n x5 -> x0, other arithmetic: 2.84 us -> none  [the longest x2 1.42 us: return_order(): jnp.take(averaged, inverse, axis=0)]
  transfers between devices with their start and end apart: 5 -> 2, of which waited for: 4 -> 2; matrix products, arithmetic and copies ran while one was open for 12% -> 5% of each run, Pallas kernels for 0% -> 0%
where the time goes in v1:
time: 64.2 us; the launch traced here: 63.8 us
  waiting for transfers between devices  38.1 us (59%)
  starting transfers between devices  11 us (17%)
  Pallas kernels  3.79 us (6%)
  between operations  3.77 us (6%)
  other arithmetic  3.7 us (6%)
  local copies, waits for them, and re-layouts  2.85 us (4%)
  matrix products  0.65 us (1%)
    all_to_all x1, waiting for transfers between devices, local(): lax.all_to_all(pieces, GRID, split_axis=0, concat_axis=0, tiled=True)  20.9 us
    all_to_all x1, waiting for transfers between devices, local(): lax.all_to_all(chosen, GRID, split_axis=0, concat_axis=0, tiled=True)  17.2 us
    all_to_all x1, starting transfers between devices, local(): lax.all_to_all(pieces, GRID, split_axis=0, concat_axis=0, tiled=True)  7.33 us
    all_to_all x1, starting transfers between devices, local(): lax.all_to_all(chosen, GRID, split_axis=0, concat_axis=0, tiled=True)  3.62 us
    pallas_call x1, Pallas kernels, local(): pl.pallas_call(mix_kernel, in_specs=[SMEM, VMEM], out_specs=(VMEM, VMEM),...  2.5 us
    mul x1, other arithmetic, local(): averaged = code * root * (bound * TOP ** (-0.5))  1.46 us
    convert_element_type x1, other arithmetic, local(): chosen = chosen.astype(jnp.float16)  1.44 us
    pallas_call x1, Pallas kernels, local(): pl.pallas_call(pack_kernel, in_specs=[SMEM, pl.BlockSpec(memory_space=pl....  1.29 us
  transfers between devices with their start and end apart: 2, of which 2 were waited for; matrix products, arithmetic and copies ran while one was open for 5% of the time, Pallas kernels for 0%

profile of v1, /device:TPU:0, one launch (start us, length us, event | category | flops | bytes accessed | tf_op | source)
XLA Modules:
  0.0 63.8 jit_solution(16474233880606717703)
XLA Ops:
  1.3 0.0 copy-start
  1.3 1.1 %copy-done = bf16[1,1,4,64,1536]{4,3,2,1,0:T(8,128)(2,1)S(1)} copy-done((bf16[1,1,4,64,1536]{4,3,2,1,0:T(8,128)(2,1)S(1)}, bf16[1,1,4,64,1536]{4,3,2,1,0:T(8,128)(2,1)}, u32[]{:S(2)}) %copy-start) | copy-done | bytes 786456
  2.4 0.0 copy-start.1
  2.4 0.0 copy-start.2
  2.4 1.3 %shard_map.59 = bf16[256,1664]{1,0:T(8,128)(2,1)} custom-call(s32[1]{0:T(128)} %bitcast.33.count, bf16[256,1536]{1,0:T(8,128)(2,1)S(1)} %bitcast.34), custom_call_target="tpu_custom_call" | custom-call | tf_op jit(solution)/shard_map/pallas_call | solution.py:101
  3.7 7.3 %all-to-all-start = ((bf16[32,8,1664]{2,1,0:T(8,128)(2,1)}), bf16[32,8,1664]{2,1,0:T(8,128)(2,1)S(1)}, u32[]{:S(2)}, u32[]{:S(2)}) async-start(bf16[32,8,1664]{2,1,0:T(8,128)(2,1)} %bitcast.8), calls=%async_computation | async-start | bytes 1703936 | tf_op jit(solution)/shard_map/all_to_all | solution.py:110
  11.1 0.0 copy-done.1
  11.1 0.1 copy.12
  11.2 0.1 convert_element_type.31
  11.3 0.0 copy-done.2
  11.3 0.2 convolution_bitcast_fusion.1
  11.5 0.2 convolution_bitcast_fusion.2
  11.7 0.1 convolution_bitcast_fusion
  11.8 0.1 fusion.3
  11.9 0.1 copy.15
  12.0 0.1 reshape.50.paths
  12.1 20.9 %all-to-all-done.pieces = bf16[32,8,1664]{2,1,0:T(8,128)(2,1)S(1)} async-done(((bf16[32,8,1664]{2,1,0:T(8,128)(2,1)}), bf16[32,8,1664]{2,1,0:T(8,128)(2,1)S(1)}, u32[]{:S(2)}, u32[]{:S(2)}) %all-to-all-start) | async-done | bytes 852000 | tf_op jit(solution)/shard_map/all_to_all | solution.py:110
  33.0 2.5 %shard_map.60 = (f32[4,8,1536]{2,1,0:T(8,128)S(1)}, f32[4,8,128]{2,1,0:T(8,128)S(1)}) custom-call(f32[4,32]{1,0:T(4,128)S(1)} %reshape.50.paths, bf16[32,8,1664]{2,1,0:T(8,128)(2,1)S(1)} %all-to-all-done.pieces), custom_call_target="tpu_custom_call" | custom-call | tf_op jit(solution)/shard_map/pallas_call | solution.py:113
  35.6 1.4 %select_convert_fusion = f16[32,8,1536]{2,1,0:T(8,128)(2,1)} fusion(f32[8,1536]{1,0:T(8,128)S(1)} %get-tuple-element.7, f32[8,1536]{1,0:T(8,128)S(1)} %get-tuple-element.8, f32[8,1536]{1,0:T(8,128)S(1)} %get-tuple-element.9, f32[8,1536]{1,0:T(8,128)S(1)} %get-tuple-element.6, pred[32]{0:T(512)(128)(4,1)S(1)} %get-tuple-element.15, ...), kind=kLoop, calls=%fused_computation.5 | loop fusion | flops 1572864 | bytes 983136 | tf_op jit(solution)/shard_map/convert_element_type | solution.py:126
  37.0 3.6 %all-to-all-start.1 = ((f16[32,8,1536]{2,1,0:T(8,128)(2,1)}), f16[32,8,1536]{2,1,0:T(8,128)(2,1)S(1)}, u32[]{:S(2)}, u32[]{:S(2)}) async-start(f16[32,8,1536]{2,1,0:T(8,128)(2,1)} %select_convert_fusion), calls=%async_computation.1 | async-start | bytes 1572864 | tf_op jit(solution)/shard_map/all_to_all | solution.py:127
  40.7 0.6 dynamic_slice.3
  41.2 0.6 %iota_compare_fusion.7 = pred[4]{0:T(512)(128)(4,1)S(1)} fusion(s32[]{:T(128)} %bitcast.13), kind=kLoop, calls=%fused_computation.27 | loop fusion | flops 4 | bytes 8 | tf_op jit(solution)/shard_map/eq | solution.py:128
  41.9 0.1 copy.16
  42.0 0.1 fusion.9
  42.1 0.7 %fusion.10 = (f32[1]{0:T(128)}, f32[1]{0:T(128)}) fusion(f32[2]{0:T(128)S(1)} %fusion.9), kind=kLoop, calls=%fused_computation.31 | loop fusion | bytes 16 | tf_op jit(solution)/shard_map/unstack | solution.py:129
  44.0 17.2 %all-to-all-done.1 = f16[32,8,1536]{2,1,0:T(8,128)(2,1)S(1)} async-done(((f16[32,8,1536]{2,1,0:T(8,128)(2,1)}), f16[32,8,1536]{2,1,0:T(8,128)(2,1)S(1)}, u32[]{:S(2)}, u32[]{:S(2)}) %all-to-all-start.1) | async-done | bytes 786464 | tf_op jit(solution)/shard_map/all_to_all | solution.py:127
  61.2 1.5 %fusion.2 = f32[32,8,1536]{2,1,0:T(8,128)} fusion(f16[32,8,1536]{2,1,0:T(8,128)(2,1)S(1)} %all-to-all-done.1, f32[]{:T(128)} %bitcast.15), kind=kLoop, calls=%fused_computation.4 | loop fusion | flops 1966080 | bytes 2359300 | tf_op jit(solution)/shard_map/mul | solution.py:132
  (7 shorter events, 0.1 us)
Async XLA Ops:
  1.3 1.1 %copy-start = (bf16[1,1,4,64,1536]{4,3,2,1,0:T(8,128)(2,1)S(1)}, bf16[1,1,4,64,1536]{4,3,2,1,0:T(8,128)(2,1)}, u32[]{:S(2)}) copy-start(bf16[1,1,4,64,1536]{4,3,2,1,0:T(8,128)(2,1)} %param.4) | copy-start | bytes 2359300
  2.4 8.6 %copy-start.1 = (s32[2,8,4]{1,2,0:T(4,128)S(1)}, s32[2,8,4]{1,2,0:T(4,128)}, u32[]{:S(2)}) copy-start(s32[2,8,4]{1,2,0:T(4,128)} %param.6) | copy-start | bytes 772
  2.4 8.9 %copy-start.2 = (s32[1,4,8]{2,1,0:T(4,128)S(1)}, s32[1,4,8]{2,1,0:T(4,128)}, u32[]{:S(2)}) copy-start(s32[1,4,8]{2,1,0:T(4,128)} %param.7) | copy-start | bytes 388
  3.7 29.3 %all-to-all-start = ((bf16[32,8,1664]{2,1,0:T(8,128)(2,1)}), bf16[32,8,1664]{2,1,0:T(8,128)(2,1)S(1)}, u32[]{:S(2)}, u32[]{:S(2)}) async-start(bf16[32,8,1664]{2,1,0:T(8,128)(2,1)} %bitcast.8), calls=%async_computation | async-start | bytes 1703936 | tf_op jit(solution)/shard_map/all_to_all | solution.py:110
  37.0 24.2 %all-to-all-start.1 = ((f16[32,8,1536]{2,1,0:T(8,128)(2,1)}), f16[32,8,1536]{2,1,0:T(8,128)(2,1)S(1)}, u32[]{:S(2)}, u32[]{:S(2)}) async-start(f16[32,8,1536]{2,1,0:T(8,128)(2,1)} %select_convert_fusion), calls=%async_computation.1 | async-start | bytes 1572864 | tf_op jit(solution)/shard_map/all_to_all | solution.py:127

commit v2 on v1

v2 whole, which is shorter than its diff:
```python
import functools

import jax
import jax.numpy as jnp
from jax import lax
from jax.experimental import pallas as pl
from jax.experimental.pallas import tpu as pltpu
from jax.sharding import PartitionSpec as P

GRID = ("row", "col")
TOP = 60000.0
TAIL = 128
CUTS = 8
SMEM = pl.BlockSpec(memory_space=pltpu.SMEM)
VMEM = pl.BlockSpec(memory_space=pltpu.VMEM)
HBM = pl.BlockSpec(memory_space=pltpu.HBM)
ROOM = pltpu.CompilerParams(vmem_limit_bytes=16 * 2**20)


def one_hot(values, count):
    return (values[..., None] == jnp.arange(count, dtype=jnp.int32)).astype(jnp.float32)


def path_counts(row_groups, col_groups):
    rows, cols = row_groups.shape[1:]
    first = one_hot(row_groups[0], cols)
    second = one_hot(col_groups[0], rows)
    third = one_hot(row_groups[1], cols)
    exact = functools.partial(jnp.einsum, precision=lax.Precision.HIGHEST)
    two = exact("jhi,igj->hg", second, first)
    three = exact("ikj,jhi->kh", third, second)
    paths = exact("kg,igj->kij", exact("kh,hg->kg", three, two), first)
    numbers = jnp.arange(cols, dtype=jnp.float32)[None, :, None]
    group_of = jnp.sum(third * numbers, axis=1).astype(jnp.int32)
    return paths.reshape(cols, rows * cols), group_of.reshape(-1)


def pack_kernel(token, gradients, out, held, tail, count, sems):
    height, width = gradients.shape
    cut = height // CUTS
    fetch = pltpu.make_async_copy(token, count, sems.at[2 * CUTS])
    fetch.start()
    arriving, leaving = [], []
    for n in range(CUTS):
        part = pl.ds(n * cut, cut)
        copy = pltpu.make_async_copy(gradients.at[part, :], held.at[part, :], sems.at[n])
        copy.start()
        arriving.append(copy)
    peak = jnp.zeros((1, width), jnp.float32)
    for n, copy in enumerate(arriving):
        part = pl.ds(n * cut, cut)
        copy.wait()
        copy = pltpu.make_async_copy(
            held.at[part, :], out.at[part, pl.ds(0, width)], sems.at[CUTS + n]
        )
        copy.start()
        leaving.append(copy)
        x = held[part, :].astype(jnp.float32)
        peak = jnp.maximum(peak, jnp.max(jnp.abs(x), axis=0, keepdims=True))
    highest = jnp.max(peak, axis=1, keepdims=True)
    fetch.wait()
    lane = lax.broadcasted_iota(jnp.int32, (height, TAIL), 1)
    facts = jnp.where(lane < TAIL // 2, count[0, 0].astype(jnp.float32), highest)
    tail[...] = facts.astype(tail.dtype)
    copy = pltpu.make_async_copy(tail, out.at[:, pl.ds(width, TAIL)], sems.at[2 * CUTS + 1])
    copy.start()
    leaving.append(copy)
    for copy in leaving:
        copy.wait()


def mix_kernel(paths, pieces, coded, facts, counts):
    groups, replicas = paths.shape
    step = 4 if replicas % 4 == 0 else 1
    stride = 32 if replicas % 32 == 0 else step
    width = pieces.shape[2] - TAIL
    height = pieces.shape[1]
    lanes = width // 2 if width % 256 == 0 else TAIL
    shape = (height, TAIL)

    def zeros(number):
        return tuple(jnp.zeros(shape, jnp.float32) for _ in range(number))

    for k0 in range(0, groups, 4):
        ks = range(k0, min(k0 + 4, groups))

        def head(s, held):
            for u in range(stride):
                at = s * stride + u
                tail = pieces[at, :, width:].astype(jnp.float32)
                w = jnp.broadcast_to(tail[:, :1], shape)
                wm = w * jnp.broadcast_to(tail[:, TAIL - 1:], shape)
                counts[at] = w
                totals, bounds = held
                totals = tuple(a + paths[k, at] * w for a, k in zip(totals, ks))
                bounds = tuple(a + paths[k, at] * wm for a, k in zip(bounds, ks))
                held = (totals, bounds)
            return held

        start = (zeros(len(ks)), zeros(len(ks)))
        totals, bounds = lax.fori_loop(0, replicas // stride, head, start)
        lane = lax.broadcasted_iota(jnp.int32, shape, 1)
        inverse = []
        for t, b, k in zip(totals, bounds, ks):
            facts[k] = jnp.where(lane == 0, t, b / t)
            inverse.append(jnp.where(b > 0.0, 1.0 / b, 0.0))
        for c in range(0, width, lanes):
            columns = range(c, c + lanes, TAIL)

            def body(s, sums):
                for u in range(step):
                    at = s * step + u
                    w = counts[at]
                    shares = tuple(paths[k, at] * w for k in ks)
                    xs = tuple(pieces[at, :, l:l + TAIL].astype(jnp.float32) for l in columns)
                    sums = tuple(
                        tuple(a + q * x for a, x in zip(line, xs)) for line, q in zip(sums, shares)
                    )
                return sums

            start = tuple(zeros(len(columns)) for _ in ks)
            sums = lax.fori_loop(0, replicas // step, body, start)
            for line, i, k in zip(sums, inverse, ks):
                for a, l in zip(line, columns):
                    unit = a * i
                    coded[k, :, l:l + TAIL] = unit * jnp.abs(unit) * TOP


def local(gradients, token_counts, row_groups, col_groups):
    rows, cols = lax.axis_size("row"), lax.axis_size("col")
    replicas = rows * cols
    place = lax.axis_index("row") * cols + lax.axis_index("col")
    width = gradients.shape[-1]
    flat = gradients.reshape(-1, width)
    packed = pl.pallas_call(
        pack_kernel,
        in_specs=[HBM, HBM],
        out_specs=HBM,
        out_shape=jax.ShapeDtypeStruct((flat.shape[0], width + TAIL), flat.dtype),
        scratch_shapes=[
            pltpu.VMEM(flat.shape, flat.dtype),
            pltpu.VMEM((flat.shape[0], TAIL), flat.dtype),
            pltpu.SMEM((1, 1), jnp.int32),
            pltpu.SemaphoreType.DMA((2 * CUTS + 2,)),
        ],
    )(token_counts, flat)
    pieces = packed.reshape(replicas, -1, width + TAIL)
    arrived = lax.all_to_all(pieces, GRID, split_axis=0, concat_axis=0, tiled=True)
    height = arrived.shape[1]
    paths, group_of = path_counts(row_groups, col_groups)
    coded, facts = pl.pallas_call(
        mix_kernel,
        in_specs=[SMEM, VMEM],
        out_specs=(VMEM, VMEM),
        out_shape=(
            jax.ShapeDtypeStruct((cols, height, width), jnp.float32),
            jax.ShapeDtypeStruct((cols, height, TAIL), jnp.float32),
        ),
        scratch_shapes=[pltpu.VMEM((replicas, height, TAIL), jnp.float32)],
        compiler_params=ROOM,
    )(paths, arrived)
    chosen = coded[0][None]
    for k in range(1, cols):
        chosen = jnp.where((group_of == k)[:, None, None], coded[k][None], chosen)
    chosen = chosen.astype(jnp.float16)
    returned = lax.all_to_all(chosen, GRID, split_axis=0, concat_axis=0, tiled=True)
    own = (jnp.arange(cols) == group_of[place])[:, None]
    total, bound = jnp.sum(jnp.where(own, facts[:, 0, :2], 0.0), axis=0)
    code = returned.astype(jnp.float32)
    root = lax.rsqrt(jnp.maximum(jnp.abs(code), 1e-12))
    averaged = code * root * (bound * TOP ** -0.5)
    return (
        averaged.reshape(gradients.shape),
        total.astype(jnp.int32).reshape(token_counts.shape),
    )


def solution(mesh):
    placed = (P(*GRID, None, None, None), P(*GRID), P(), P())
    return jax.shard_map(
        local,
        mesh=mesh,
        in_specs=placed,
        out_specs=(P(*GRID, None, None, None), P(*GRID)),
        check_vma=False,
    )
```

time: 64.2 us -> 62.9 us (0.980)
  local copies, waits for them, and re-layouts: 2.85 us -> 1.66 us
    unnamed x6 -> x4, local copies, waits for them, and re-layouts: 1.13 us -> 0.01 us
    pallas_call x1, Pallas kernels: 2.5 us -> 1.51 us  [local(): pl.pallas_call(mix_kernel, in_specs=[SMEM, VMEM], out_specs=(VMEM, VMEM),...]
    pallas_call x1, Pallas kernels: 1.29 us -> 2.13 us  [local(): pl.pallas_call(pack_kernel, in_specs=[HBM, HBM], out_specs=HBM, out_shape...]
where the time goes in v2:
time: 62.9 us; the launch traced here: 62.5 us
  waiting for transfers between devices  38.2 us (61%)
  starting transfers between devices  11 us (17%)
  between operations  3.78 us (6%)
  other arithmetic  3.7 us (6%)
  Pallas kernels  3.64 us (6%)
  local copies, waits for them, and re-layouts  1.66 us (3%)
  matrix products  0.65 us (1%)
    all_to_all x1, waiting for transfers between devices, local(): lax.all_to_all(pieces, GRID, split_axis=0, concat_axis=0, tiled=True)  20.9 us
    all_to_all x1, waiting for transfers between devices, local(): lax.all_to_all(chosen, GRID, split_axis=0, concat_axis=0, tiled=True)  17.3 us
    all_to_all x1, starting transfers between devices, local(): lax.all_to_all(pieces, GRID, split_axis=0, concat_axis=0, tiled=True)  7.33 us
    all_to_all x1, starting transfers between devices, local(): lax.all_to_all(chosen, GRID, split_axis=0, concat_axis=0, tiled=True)  3.62 us
    pallas_call x1, Pallas kernels, local(): pl.pallas_call(pack_kernel, in_specs=[HBM, HBM], out_specs=HBM, out_shape...  2.13 us
    pallas_call x1, Pallas kernels, local(): pl.pallas_call(mix_kernel, in_specs=[SMEM, VMEM], out_specs=(VMEM, VMEM),...  1.51 us
    mul x1, other arithmetic, local(): averaged = code * root * (bound * TOP ** (-0.5))  1.46 us
    convert_element_type x1, other arithmetic, local(): chosen = chosen.astype(jnp.float16)  1.44 us
  transfers between devices with their start and end apart: 2, of which 2 were waited for; matrix products, arithmetic and copies ran while one was open for 5% of the time, Pallas kernels for 0%

profile of v2, /device:TPU:0, one launch (start us, length us, event | category | flops | bytes accessed | tf_op | source)
XLA Modules:
  0.0 62.5 jit_solution(12660493882281563723)
XLA Ops:
  1.3 0.0 copy-start
  1.3 0.0 copy-start.1
  1.3 2.1 %shard_map.59 = bf16[256,1664]{1,0:T(8,128)(2,1)} custom-call(s32[1,1]{1,0:T(1,128)S(6)} %copy.22.token, bf16[256,1536]{1,0:T(8,128)(2,1)} %bitcast.34), custom_call_target="tpu_custom_call" | custom-call | tf_op jit(solution)/shard_map/pallas_call | solution.py:135
  3.4 7.3 %all-to-all-start = ((bf16[32,8,1664]{2,1,0:T(8,128)(2,1)}), bf16[32,8,1664]{2,1,0:T(8,128)(2,1)S(1)}, u32[]{:S(2)}, u32[]{:S(2)}) async-start(bf16[32,8,1664]{2,1,0:T(8,128)(2,1)} %bitcast.32), calls=%async_computation | async-start | bytes 1703936 | tf_op jit(solution)/shard_map/all_to_all | solution.py:148
  10.8 0.0 copy-done
  10.8 0.1 copy.12
  10.9 0.1 convert_element_type.31
  11.0 0.0 copy-done.1
  11.0 0.2 convolution_bitcast_fusion.1
  11.2 0.2 convolution_bitcast_fusion.2
  11.4 0.1 convolution_bitcast_fusion
  11.5 0.1 fusion.3
  11.6 0.1 copy.15
  11.7 0.1 reshape.47.paths
  11.8 20.9 %all-to-all-done.pieces = bf16[32,8,1664]{2,1,0:T(8,128)(2,1)S(1)} async-done(((bf16[32,8,1664]{2,1,0:T(8,128)(2,1)}), bf16[32,8,1664]{2,1,0:T(8,128)(2,1)S(1)}, u32[]{:S(2)}, u32[]{:S(2)}) %all-to-all-start) | async-done | bytes 852000 | tf_op jit(solution)/shard_map/all_to_all | solution.py:148
  32.8 1.5 %shard_map.60 = (f32[4,8,1536]{2,1,0:T(8,128)S(1)}, f32[4,8,128]{2,1,0:T(8,128)S(1)}) custom-call(f32[4,32]{1,0:T(4,128)S(1)} %reshape.47.paths, bf16[32,8,1664]{2,1,0:T(8,128)(2,1)S(1)} %all-to-all-done.pieces), custom_call_target="tpu_custom_call" | custom-call | tf_op jit(solution)/shard_map/pallas_call | solution.py:151
  34.3 1.4 %select_convert_fusion = f16[32,8,1536]{2,1,0:T(8,128)(2,1)} fusion(f32[8,1536]{1,0:T(8,128)S(1)} %get-tuple-element.7, f32[8,1536]{1,0:T(8,128)S(1)} %get-tuple-element.8, f32[8,1536]{1,0:T(8,128)S(1)} %get-tuple-element.9, f32[8,1536]{1,0:T(8,128)S(1)} %get-tuple-element.6, pred[32]{0:T(512)(128)(4,1)S(1)} %get-tuple-element.15, ...), kind=kLoop, calls=%fused_computation.5 | loop fusion | flops 1572864 | bytes 983136 | tf_op jit(solution)/shard_map/convert_element_type | solution.py:165
  35.7 3.6 %all-to-all-start.1 = ((f16[32,8,1536]{2,1,0:T(8,128)(2,1)}), f16[32,8,1536]{2,1,0:T(8,128)(2,1)S(1)}, u32[]{:S(2)}, u32[]{:S(2)}) async-start(f16[32,8,1536]{2,1,0:T(8,128)(2,1)} %select_convert_fusion), calls=%async_computation.1 | async-start | bytes 1572864 | tf_op jit(solution)/shard_map/all_to_all | solution.py:166
  39.4 0.6 dynamic_slice.3
  40.0 0.6 %iota_compare_fusion.7 = pred[4]{0:T(512)(128)(4,1)S(1)} fusion(s32[]{:T(128)} %bitcast.12), kind=kLoop, calls=%fused_computation.27 | loop fusion | flops 4 | bytes 8 | tf_op jit(solution)/shard_map/eq | solution.py:167
  40.6 0.1 copy.16
  40.7 0.1 fusion.9
  40.8 0.6 fusion.10
  42.7 17.3 %all-to-all-done.1 = f16[32,8,1536]{2,1,0:T(8,128)(2,1)S(1)} async-done(((f16[32,8,1536]{2,1,0:T(8,128)(2,1)}), f16[32,8,1536]{2,1,0:T(8,128)(2,1)S(1)}, u32[]{:S(2)}, u32[]{:S(2)}) %all-to-all-start.1) | async-done | bytes 786464 | tf_op jit(solution)/shard_map/all_to_all | solution.py:166
  60.0 1.5 %fusion.2 = f32[32,8,1536]{2,1,0:T(8,128)} fusion(f16[32,8,1536]{2,1,0:T(8,128)(2,1)S(1)} %all-to-all-done.1, f32[]{:T(128)} %bitcast.14), kind=kLoop, calls=%fused_computation.4 | loop fusion | flops 1966080 | bytes 2359300 | tf_op jit(solution)/shard_map/mul | solution.py:171
  (7 shorter events, 0.1 us)
Async XLA Ops:
  1.3 9.5 %copy-start = (s32[2,8,4]{1,2,0:T(4,128)S(1)}, s32[2,8,4]{1,2,0:T(4,128)}, u32[]{:S(2)}) copy-start(s32[2,8,4]{1,2,0:T(4,128)} %param.6) | copy-start | bytes 772
  1.3 9.7 %copy-start.1 = (s32[1,4,8]{2,1,0:T(4,128)S(1)}, s32[1,4,8]{2,1,0:T(4,128)}, u32[]{:S(2)}) copy-start(s32[1,4,8]{2,1,0:T(4,128)} %param.7) | copy-start | bytes 388
  3.4 29.3 %all-to-all-start = ((bf16[32,8,1664]{2,1,0:T(8,128)(2,1)}), bf16[32,8,1664]{2,1,0:T(8,128)(2,1)S(1)}, u32[]{:S(2)}, u32[]{:S(2)}) async-start(bf16[32,8,1664]{2,1,0:T(8,128)(2,1)} %bitcast.32), calls=%async_computation | async-start | bytes 1703936 | tf_op jit(solution)/shard_map/all_to_all | solution.py:148
  35.7 24.2 %all-to-all-start.1 = ((f16[32,8,1536]{2,1,0:T(8,128)(2,1)}), f16[32,8,1536]{2,1,0:T(8,128)(2,1)S(1)}, u32[]{:S(2)}, u32[]{:S(2)}) async-start(f16[32,8,1536]{2,1,0:T(8,128)(2,1)} %select_convert_fusion), calls=%async_computation.1 | async-start | bytes 1572864 | tf_op jit(solution)/shard_map/all_to_all | solution.py:166
